TPU v7x, 32 devices: a whole 2x2x4 slice. The times are simulated.
32 devices in a mesh: row: 4 (over y, x), col: 8 (over z, core).
Axes of the slice: x: 2, y: 2, z: 4, core: 2. Of those that a mesh axis runs over, the one named last changes fastest.
Arguments:
- features: bfloat16 [8192, 512], P(('row', 'col')), may hold values from -6 to 6
- tile_values: bfloat16 [4, 8, 128, 128, 128], P('row', 'col'), may hold values from -0.1875 to 0.1875
- tile_places: int32 [4, 8, 2, 128], P('row', 'col'), may hold values from 0 to 15, as said below
- tile_counts: int32 [4, 8], replicated, may hold values from 40 to 128, as said below
- weight_one: float32 [512, 512], replicated, may hold values from -0.25 to 0.25
- weight_two: float32 [512, 512], replicated, may hold values from -0.25 to 0.25
Outputs:
- embedded: float32 [8192, 512], P(('row', 'col'))
Inputs may be any that keep to these rules, and one draw needn't show every extreme that they name: `tile_places`: in every block the first tile_counts slots name distinct tiles with tile rows below 16 and tile columns below 8, listed in order of tile row (never falling); later slots also name tiles in range. `tile_counts`: some block has exactly 128 tiles.
All inputs are finite; a program needn't handle non-finite values.
Results may differ from a plain program's by a relative error of at most 0.0029.
Values may be sent and summed in bfloat16 or wider, within the bound.
A program may use at most 64 MiB of HBM per device.

v0:
```python
import functools

import jax
import jax.numpy as jnp
from jax import lax
from jax.experimental import pallas as pl
from jax.experimental.pallas import tpu as pltpu
from jax.sharding import PartitionSpec as P

MESH = pl.DeviceIdType.MESH
PARTS = 4
LINK_TYPES = (jnp.int16, jnp.bfloat16)
TOP = 32766.0
SKEW = 2


def kernel(
    n_row, n_col,
    counts_ref, places_ref, features_ref, tiles_hbm, weight_one_hbm, weight_two_hbm,
    out_ref,
    tiles, dense, weights, hidden, inputs, own, total,
    pair_out, pair_in, up_out0, up_in0, down_out0, down_in0, up_out1, up_in1, down_out1, down_in1,
    scale_up_out, scale_up_in, scale_down_out, scale_down_in,
    load_sem, gather_send, gather_recv, pair_send, pair_recv, up_send, up_recv, down_send, down_recv,
    scale_send, scale_recv,
    inverse_rows, inverse_ref,
):
    row, col = lax.axis_index("row"), lax.axis_index("col")
    n_chip = n_col // 2
    chip, core = col // 2, col % 2
    partner = chip * 2 + (1 - core)
    slots, tile = tiles_hbm.shape[0], tiles_hbm.shape[1]
    piece, width = features_ref.shape
    part = width // PARTS
    tile_rows, tile_cols = dense.shape[0] // tile, dense.shape[1] // tile

    tile_load = pltpu.make_async_copy(tiles_hbm, tiles.at[pl.ds(0, slots)], load_sem.at[0])
    tile_load.start()
    weight_loads = [
        pltpu.make_async_copy(weight_one_hbm, weights.at[0], load_sem.at[1]),
        pltpu.make_async_copy(weight_two_hbm, weights.at[1], load_sem.at[2]),
    ]
    for load in weight_loads:
        load.start()

    barrier = pltpu.get_barrier_semaphore()
    for step in range(1, n_row):
        pl.semaphore_signal(
            barrier, inc=1, device_id=(lax.rem(row + step, n_row), col), device_id_type=MESH
        )
    pl.semaphore_signal(barrier, inc=1, device_id=(row, partner), device_id_type=MESH)

    @pl.when(chip > 0)
    def _():
        pl.semaphore_signal(barrier, inc=1, device_id=(row, col - 2), device_id_type=MESH)

    @pl.when(chip < n_chip - 1)
    def _():
        pl.semaphore_signal(barrier, inc=1, device_id=(row, col + 2), device_id_type=MESH)

    peers = n_row + jnp.where(chip > 0, 1, 0) + jnp.where(chip < n_chip - 1, 1, 0)
    pl.semaphore_wait(barrier, peers)

    def gather_copy(layer, source, h, step):
        return pltpu.make_async_remote_copy(
            src_ref=source.at[:, pl.ds(h * part, part)],
            dst_ref=inputs.at[layer, h, pl.ds(pl.multiple_of(row * piece, piece), piece), :],
            send_sem=gather_send.at[layer, h, step - 1],
            recv_sem=gather_recv.at[layer, h, step - 1],
            device_id=(lax.rem(row + step, n_row), col),
            device_id_type=MESH,
        )

    def pair_copy(layer, h, d):
        return pltpu.make_async_remote_copy(
            src_ref=pair_out.at[layer, h, d],
            dst_ref=pair_in.at[layer, h, d],
            send_sem=pair_send.at[layer, h, d],
            recv_sem=pair_recv.at[layer, h, d],
            device_id=(row, partner),
            device_id_type=MESH,
        )

    ups = ((up_out0, up_in0), (up_out1, up_in1))
    downs = ((down_out0, down_in0), (down_out1, down_in1))

    def up_copy(layer, h, j):
        return pltpu.make_async_remote_copy(
            src_ref=ups[layer][0].at[h, j],
            dst_ref=ups[layer][1].at[h, j],
            send_sem=up_send.at[layer, h, j],
            recv_sem=up_recv.at[layer, h, j],
            device_id=(row, col + 2),
            device_id_type=MESH,
        )

    def down_copy(layer, h, j):
        return pltpu.make_async_remote_copy(
            src_ref=downs[layer][0].at[h, j],
            dst_ref=downs[layer][1].at[h, j],
            send_sem=down_send.at[layer, h, j],
            recv_sem=down_recv.at[layer, h, j],
            device_id=(row, col - 2),
            device_id_type=MESH,
        )

    scales = ((scale_up_out, scale_up_in), (scale_down_out, scale_down_in))

    def scale_copy(way, h, j):
        return pltpu.make_async_remote_copy(
            src_ref=scales[way][0].at[h, j],
            dst_ref=scales[way][1].at[h, j],
            send_sem=scale_send.at[way, h, j],
            recv_sem=scale_recv.at[way, h, j],
            device_id=(row, col + 2 if way == 0 else col - 2),
            device_id_type=MESH,
        )

    def flow_copy(layer, way, h, j):
        return (up_copy, down_copy)[way](layer, h, j)

    def flow_send(layer, way, h, j, value):
        target = (ups, downs)[way][layer][0]
        if LINK_TYPES[layer] == jnp.int16:
            peak = jnp.maximum(jnp.max(jnp.abs(value), axis=0, keepdims=True), 1e-30)
            scales[way][0][h, j] = jnp.broadcast_to(peak * (1.0 / TOP), scales[way][0].shape[2:])
            scale_copy(way, h, j).start()
            target[h, j] = jnp.round(value * (TOP / peak)).astype(jnp.int32).astype(jnp.int16)
        else:
            target[h, j] = value.astype(target.dtype)
        flow_copy(layer, way, h, j).start()

    def flow_take(layer, way, h, j):
        source = (ups, downs)[way][layer][1]
        flow_copy(layer, way, h, j).wait_recv()
        if LINK_TYPES[layer] == jnp.int16:
            scale_copy(way, h, j).wait_recv()
            return source[h, j].astype(jnp.int32).astype(jnp.float32) * scales[way][1][h, j, 0:1, :]
        return source[h, j].astype(jnp.float32)

    def flow_drain(layer, way, h, j):
        flow_copy(layer, way, h, j).wait_send()
        if LINK_TYPES[layer] == jnp.int16:
            scale_copy(way, h, j).wait_send()

    def pair_sum(layer, h, d):
        pair_copy(layer, h, d).wait_recv()
        return own[h, d] + pair_in[layer, h, d]

    def send_up(layer, h, j, first):
        d = n_chip - 1 - j

        @pl.when(d > chip)
        def _():
            value = pair_sum(layer, h, d)
            if not first:
                value = value + flow_take(layer, 0, h, j)
            flow_send(layer, 0, h, j, value)

    def send_down(layer, h, j, first):
        d = j

        @pl.when(d < chip)
        def _():
            value = pair_sum(layer, h, d)
            if not first:
                value = value + flow_take(layer, 1, h, j)
            flow_send(layer, 1, h, j, value)

    def start_gather(layer, source):
        for h in range(PARTS):
            for step in range(1, n_row):
                gather_copy(layer, source, h, step).start()
        for h in range(PARTS):
            inputs[layer, h, pl.ds(pl.multiple_of(row * piece, piece), piece), :] = source[
                :, h * part : (h + 1) * part
            ]

    def chunk(layer, h, index):
        rows = pl.ds(pl.multiple_of(index * piece, piece), piece)
        return jnp.dot(dense[rows, :], inputs[layer, h], preferred_element_type=jnp.float32)

    def aggregate(layer, source):
        turns = n_chip - 1
        steps = PARTS * turns

        def forward(time, carry):
            for send, hops in ((send_up, chip), (send_down, turns - chip)):
                step = time - SKEW * hops

                @pl.when((step >= 0) & (step < steps) & (hops > 0))
                def _():
                    send(layer, step // turns, step % turns, False)

            return carry

        for h in range(PARTS):
            for step in range(1, n_row):
                gather_copy(layer, source, h, step).wait_recv()

            def one_chunk(i, carry):
                d = jnp.where(i % 2 == 0, n_chip - 1 - i // 2, i // 2)
                pair_out[layer, h, d] = chunk(layer, h, d * 2 + (1 - core))
                pair_copy(layer, h, d).start()
                own[h, d] = chunk(layer, h, d * 2 + core)
                return carry

            lax.fori_loop(0, n_chip, one_chunk, 0)

            @pl.when(chip == 0)
            def _():
                lax.fori_loop(0, n_chip - 1, lambda j, c: (send_up(layer, h, j, True), c)[1], 0)

            @pl.when(chip == n_chip - 1)
            def _():
                lax.fori_loop(0, n_chip - 1, lambda j, c: (send_down(layer, h, j, True), c)[1], 0)

            lax.fori_loop(h * turns, (h + 1) * turns, forward, 0)

        lax.fori_loop(steps, steps + SKEW * turns, forward, 0)
        for h in range(PARTS):
            columns = slice(h * part, (h + 1) * part)
            total[:, columns] = pair_sum(layer, h, chip)

            @pl.when(chip > 0)
            def _():
                total[:, columns] += flow_take(layer, 0, h, n_chip - 1 - chip)

            @pl.when(chip < n_chip - 1)
            def _():
                total[:, columns] += flow_take(layer, 1, h, chip)

    def project(layer):
        return jnp.dot(
            total[...], weights[layer], precision=lax.Precision.HIGHEST,
            preferred_element_type=jnp.float32,
        )

    start_gather(0, features_ref)
    tiles[slots] = jnp.zeros((tile, tile), tiles.dtype)
    spots = tile_rows * tile_cols
    count = counts_ref[row, col]
    order = lax.broadcasted_iota(jnp.int32, (spots, slots), 1)
    spot = lax.broadcasted_iota(jnp.int32, (spots, slots), 0)
    place = places_ref[0:1, :] * tile_cols + places_ref[1:2, :]
    listed = (place == spot) & (order < count)
    marks = jnp.where(listed, order - slots, 0)
    found = jnp.sum(marks.T, axis=0, keepdims=True) + slots
    inverse_rows[...] = jnp.broadcast_to(found, inverse_rows.shape)
    inverse_load = pltpu.make_async_copy(inverse_rows, inverse_ref, load_sem.at[3])
    inverse_load.start()
    inverse_load.wait()
    tile_load.wait()

    def place_row(i, carry):
        rows = pl.ds(pl.multiple_of(i * tile, tile), tile)
        for t in range(tile_cols):
            slot = jnp.clip(inverse_ref[0, i * tile_cols + t], 0, slots)
            dense[rows, t * tile : (t + 1) * tile] = tiles[slot]
        return carry

    lax.fori_loop(0, tile_rows, place_row, 0)
    for load in weight_loads:
        load.wait()

    aggregate(0, features_ref)
    hidden[...] = jnp.maximum(project(0), 0.0).astype(hidden.dtype)
    start_gather(1, hidden)
    aggregate(1, hidden)
    out_ref[...] = project(1)

    for layer, source in enumerate((features_ref, hidden)):
        for h in range(PARTS):
            for step in range(1, n_row):
                gather_copy(layer, source, h, step).wait_send()

            def drain_pair(d, carry):
                pair_copy(layer, h, d).wait_send()
                return carry

            lax.fori_loop(0, n_chip, drain_pair, 0)

            def drain(j, carry):
                @pl.when(n_chip - 1 - j > chip)
                def _():
                    flow_drain(layer, 0, h, j)

                @pl.when(j < chip)
                def _():
                    flow_drain(layer, 1, h, j)

                return carry

            lax.fori_loop(0, n_chip - 1, drain, 0)


def shards(n_row, n_col, features, tile_values, tile_places, tile_counts, weight_one, weight_two):
    tiles = tile_values.reshape(tile_values.shape[2:])
    places = tile_places.reshape(tile_places.shape[2:])
    slots, tile = tiles.shape[0], tiles.shape[1]
    piece, width = features.shape
    part = width // PARTS
    rows, depth = piece * n_col, piece * n_row
    tile_rows, tile_cols = rows // tile, depth // tile
    n_chip = n_col // 2
    spots = tile_rows * tile_cols

    def flow(layer):
        return pltpu.VMEM((PARTS, n_chip - 1, piece, part), LINK_TYPES[layer])

    scale = pltpu.VMEM((PARTS, n_chip - 1, 8, part), jnp.float32)
    dma = pltpu.SemaphoreType.DMA
    any_space = pl.BlockSpec(memory_space=pl.ANY)
    vmem = pl.BlockSpec(memory_space=pltpu.VMEM)
    second = pl.pallas_call(
        functools.partial(kernel, n_row, n_col),
        out_shape=jax.ShapeDtypeStruct((piece, width), jnp.float32),
        in_specs=[pl.BlockSpec(memory_space=pltpu.SMEM), vmem, vmem, any_space, any_space, any_space],
        out_specs=vmem,
        scratch_shapes=[
            pltpu.VMEM((slots + 1, tile, tile), jnp.bfloat16),
            pltpu.VMEM((rows, depth), jnp.bfloat16),
            pltpu.VMEM((2, width, width), jnp.float32),
            pltpu.VMEM((piece, width), jnp.bfloat16),
            pltpu.VMEM((2, PARTS, depth, part), jnp.bfloat16),
            pltpu.VMEM((PARTS, n_chip, piece, part), jnp.float32),
            pltpu.VMEM((piece, width), jnp.float32),
            pltpu.VMEM((2, PARTS, n_chip, piece, part), jnp.float32),
            pltpu.VMEM((2, PARTS, n_chip, piece, part), jnp.float32),
            flow(0), flow(0), flow(0), flow(0), flow(1), flow(1), flow(1), flow(1),
            scale, scale, scale, scale,
            dma((4,)),
            dma((2, PARTS, n_row - 1)), dma((2, PARTS, n_row - 1)),
            dma((2, PARTS, n_chip)), dma((2, PARTS, n_chip)),
            dma((2, PARTS, n_chip - 1)), dma((2, PARTS, n_chip - 1)),
            dma((2, PARTS, n_chip - 1)), dma((2, PARTS, n_chip - 1)),
            dma((2, PARTS, n_chip - 1)), dma((2, PARTS, n_chip - 1)),
            pltpu.VMEM((8, spots), jnp.int32), pltpu.SMEM((8, spots), jnp.int32),
        ],
        compiler_params=pltpu.CompilerParams(
            collective_id=0, has_side_effects=True, vmem_limit_bytes=60 * 1024 * 1024
        ),
    )(tile_counts, places, features, tiles, weight_one, weight_two)
    return jnp.maximum(second, 0.0)


def solution(mesh):
    placed = (
        P(("row", "col"), None),
        P("row", "col", None, None, None),
        P("row", "col", None, None),
        P(),
        P(),
        P(),
    )
    return jax.shard_map(
        functools.partial(shards, mesh.shape["row"], mesh.shape["col"]),
        mesh=mesh, in_specs=placed, out_specs=P(("row", "col"), None), check_vma=False,
    )
```

profile of v0, /device:TPU:0, one launch (start us, length us, event | category | flops | bytes accessed | tf_op | source)
XLA Modules:
  0.0 76.4 jit_solution(17292808601533919245)
XLA Ops:
  0.0 74.5 %shard_map.64 = f32[256,512]{1,0:T(8,128)} custom-call(s32[4,8]{1,0:T(4,128)} %counts_ref.1, s32[2,128]{1,0:T(2,128)} %bitcast.3, bf16[256,512]{1,0:T(8,128)(2,1)} %features_ref.1, bf16[128,128,128]{2,1,0:T(8,128)(2,1)} %bitcast.2, f32[512,512]{1,0:T(8,128)} %weight_one_hbm.1, f32[512,512]{1,0:T(8,128)} %weight_two_hbm.1), custom_call_target="tpu_custom_call" | custom-call | tf_op jit(solution)/shard_map/pallas_call | solution.py:315
  74.6 1.9 %broadcast_maximum_fusion = f32[256,512]{1,0:T(8,128)} fusion(f32[256,512]{1,0:T(8,128)} %shard_map.64), kind=kLoop, calls=%fused_computation | loop fusion | flops 131072 | bytes 1048576 | tf_op jit(solution)/shard_map/max | solution.py:344
where the time goes:
time: 76.6 us; the launch traced here: 76.4 us
  Pallas kernels  74.5 us (97%)
  other arithmetic  1.88 us (2%)
    pallas_call x1, Pallas kernels, shards(): pl.pallas_call(functools.partial(kernel, n_row, n_col), out_shape=jax.Sha...  74.5 us
    max x1, other arithmetic, shards(): return jnp.maximum(second, 0.0)  1.88 us

commit v1 on v0

v1 whole, which is shorter than its diff:
```python
import functools

import jax
import jax.numpy as jnp
from jax import lax
from jax.experimental import pallas as pl
from jax.experimental.pallas import tpu as pltpu
from jax.sharding import PartitionSpec as P

MESH = pl.DeviceIdType.MESH
PARTS = 4
LINK_TYPES = (jnp.int16, jnp.bfloat16)
TOP = 32766.0
SKEW = 3
LEAD = 2


def kernel(
    n_row, n_col, blocks,
    counts_hbm, places_hbm, features_hbm, tiles_hbm, weight_one_hbm, weight_two_hbm,
    out_hbm,
    tiles, dense, weights, inputs, total, result, prod, pair_in,
    up_out0, up_in0, down_out0, down_in0, up_out1, up_in1, down_out1, down_in1,
    scale_out, scale_in,
    load_sem, feature_sem, out_sem, near_send, near_recv, far_send, far_recv, pair_send, pair_recv,
    flow_send_sem, flow_recv_sem, scale_send, scale_recv,
    counts, places, inverse_rows, inverse_ref,
):
    row, col = lax.axis_index("row"), lax.axis_index("col")
    n_chip = n_col // 2
    chip, core = col // 2, col % 2
    partner = chip * 2 + (1 - core)
    slots, tile = tiles_hbm.shape[0], tiles_hbm.shape[1]
    piece, width = features_hbm.shape
    part = width // PARTS
    sub = piece // blocks
    depth = piece * n_row
    tile_rows, tile_cols = dense.shape[0] // tile, depth // tile
    turns = n_chip - 1
    first = PARTS * turns
    steps = blocks * first
    bits = [1 << i for i in range((n_row - 1).bit_length())]
    masks = sorted((m for m in range(1, n_row) if m & (m - 1)), key=lambda m: bin(m).count("1"))

    barrier = pltpu.get_barrier_semaphore()
    for bit in bits:
        pl.semaphore_signal(barrier, inc=1, device_id=(row ^ bit, col), device_id_type=MESH)
    pl.semaphore_signal(barrier, inc=1, device_id=(row, partner), device_id_type=MESH)

    @pl.when(chip > 0)
    def _():
        pl.semaphore_signal(barrier, inc=1, device_id=(row, col - 2), device_id_type=MESH)

    @pl.when(chip < n_chip - 1)
    def _():
        pl.semaphore_signal(barrier, inc=1, device_id=(row, col + 2), device_id_type=MESH)

    def slot_rows(b, q):
        return pl.ds(pl.multiple_of((b * n_row + q) * sub, sub), sub)

    feature_loads = [
        [
            pltpu.make_async_copy(
                features_hbm.at[pl.ds(b * sub, sub), pl.ds(h * part, part)],
                inputs.at[0, h, slot_rows(b, row), :],
                feature_sem.at[b, h],
            )
            for b in range(blocks)
        ]
        for h in range(PARTS)
    ]
    for loads in feature_loads:
        for load in loads:
            load.start()
    counts_load = pltpu.make_async_copy(counts_hbm, counts, load_sem.at[4])
    counts_load.start()
    places_load = pltpu.make_async_copy(places_hbm, places, load_sem.at[5])
    places_load.start()
    tile_load = pltpu.make_async_copy(tiles_hbm, tiles.at[pl.ds(0, slots)], load_sem.at[0])
    tile_load.start()
    weight_loads = [
        pltpu.make_async_copy(weight_one_hbm, weights.at[0], load_sem.at[1]),
        pltpu.make_async_copy(weight_two_hbm, weights.at[1], load_sem.at[2]),
    ]
    for load in weight_loads:
        load.start()

    peers = len(bits) + 1 + jnp.where(chip > 0, 1, 0) + jnp.where(chip < n_chip - 1, 1, 0)

    def near_copy(layer, b, h, i):
        block = inputs.at[layer, h, slot_rows(b, row), :]
        return pltpu.make_async_remote_copy(
            src_ref=block, dst_ref=block,
            send_sem=near_send.at[layer, b, h, i], recv_sem=near_recv.at[layer, b, h, i],
            device_id=(row ^ bits[i], col), device_id_type=MESH,
        )

    half = sub // 2

    def far_copy(layer, b, h, i, side):
        mask = masks[i]
        last = 1 << (mask.bit_length() - 1) if side == 0 else mask & -mask
        origin = row ^ (mask ^ last)
        rows = pl.ds(pl.multiple_of((b * n_row + origin) * sub + side * half, half), half)
        block = inputs.at[layer, h, rows, :]
        return pltpu.make_async_remote_copy(
            src_ref=block, dst_ref=block,
            send_sem=far_send.at[layer, b, h, i, side], recv_sem=far_recv.at[layer, b, h, i, side],
            device_id=(row ^ last, col), device_id_type=MESH,
        )

    def near_start(layer, some, h):
        for b in some:
            for i in range(len(bits)):
                near_copy(layer, b, h, i).start()

    def far_start(layer, some, h, level):
        for b in some:
            for i, mask in enumerate(masks):
                if bin(mask).count("1") == level:
                    for side in (0, 1):
                        far_copy(layer, b, h, i, side).start()

    def relay(layer, some, h):
        for b in some:
            for i in range(len(bits)):
                near_copy(layer, b, h, i).wait_recv()
        far_start(layer, some, h, 2)

    def arrive(layer, some, h):
        for level in range(2, len(bits) + 1):
            for b in some:
                for i, mask in enumerate(masks):
                    if bin(mask).count("1") == level:
                        for side in (0, 1):
                            far_copy(layer, b, h, i, side).wait_recv()
            if level < len(bits):
                far_start(layer, some, h, level + 1)

    def pair_copy(layer, h, d):
        return pltpu.make_async_remote_copy(
            src_ref=prod.at[layer, h, d, 1 - core],
            dst_ref=pair_in.at[layer, h, d],
            send_sem=pair_send.at[layer, h, d], recv_sem=pair_recv.at[layer, h, d],
            device_id=(row, partner), device_id_type=MESH,
        )

    flows = (
        ((up_out0, up_in0), (down_out0, down_in0)),
        ((up_out1, up_in1), (down_out1, down_in1)),
    )

    def flow_copy(layer, way, k):
        out_buffer, in_buffer = flows[layer][way]
        return pltpu.make_async_remote_copy(
            src_ref=out_buffer.at[k], dst_ref=in_buffer.at[k],
            send_sem=flow_send_sem.at[layer, way, k], recv_sem=flow_recv_sem.at[layer, way, k],
            device_id=(row, col + 2 if way == 0 else col - 2), device_id_type=MESH,
        )

    def scale_copy(way, k):
        return pltpu.make_async_remote_copy(
            src_ref=scale_out.at[way, k], dst_ref=scale_in.at[way, k],
            send_sem=scale_send.at[way, k], recv_sem=scale_recv.at[way, k],
            device_id=(row, col + 2 if way == 0 else col - 2), device_id_type=MESH,
        )

    def flow_send(layer, way, k, value):
        target = flows[layer][way][0]
        if LINK_TYPES[layer] == jnp.int16:
            peak = jnp.maximum(jnp.max(jnp.abs(value), axis=0, keepdims=True), 1e-30)
            scale_out[way, k] = peak * (1.0 / TOP)
            scale_copy(way, k).start()
            target[k] = jnp.round(value * (TOP / peak)).astype(jnp.int32).astype(jnp.int16)
        else:
            target[k] = value.astype(target.dtype)
        flow_copy(layer, way, k).start()

    def flow_take(layer, way, k):
        source = flows[layer][way][1]
        flow_copy(layer, way, k).wait_recv()
        if LINK_TYPES[layer] == jnp.int16:
            scale_copy(way, k).wait_recv()
            return source[k].astype(jnp.int32).astype(jnp.float32) * scale_in[way, k]
        return source[k].astype(jnp.float32)

    def pair_sum(layer, b, h, d):
        rows = pl.ds(pl.multiple_of(b * sub, sub), sub)
        return prod[layer, h, d, core, rows, :] + pair_in[layer, h, d, rows, :]

    def place_of(k):
        k = jnp.clip(k, 0, steps - 1)
        later = jnp.maximum(k - first, 0)
        b = jnp.where(k < first, 0, 1 + later // first)
        rest = lax.rem(later, first)
        h = jnp.where(k < first, k // turns, lax.rem(rest, PARTS))
        j = jnp.where(k < first, lax.rem(k, turns), rest // PARTS)
        return b, h, j

    def order_of(b, h, j):
        return h * turns + j if b == 0 else b * first + j * PARTS + h

    def send_step(layer, t):
        for way in (0, 1):
            hops = chip if way == 0 else turns - chip
            k = t - SKEW * hops
            b, h, j = place_of(k)
            d = turns - j if way == 0 else j
            ahead = d > chip if way == 0 else d < chip

            @pl.when((k >= 0) & (k < steps) & ahead)
            def _():
                @pl.when(b == 0)
                def _():
                    pair_copy(layer, h, d).wait_recv()

                @pl.when(hops == 0)
                def _():
                    flow_send(layer, way, k, pair_sum(layer, b, h, d))

                @pl.when(hops > 0)
                def _():
                    flow_send(
                        layer, way, k, pair_sum(layer, b, h, d) + flow_take(layer, way, k)
                    )

    def settle(layer, b):
        for h in range(PARTS):
            columns = slice(h * part, (h + 1) * part)
            if b == 0:
                pair_copy(layer, h, chip).wait_recv()
            total[b, :, columns] = pair_sum(layer, b, h, chip)

            @pl.when(chip > 0)
            def _():
                k = b * first + h + PARTS * (turns - chip) if b else h * turns + turns - chip
                total[b, :, columns] += flow_take(layer, 0, k)

            @pl.when(chip < turns)
            def _():
                k = b * first + h + PARTS * chip if b else h * turns + chip
                total[b, :, columns] += flow_take(layer, 1, k)

    def project(layer, b):
        return jnp.dot(
            total[b], weights[layer], precision=lax.Precision.HIGHEST,
            preferred_element_type=jnp.float32,
        )

    def chip_rows(d):
        return pl.ds(pl.multiple_of(d * (2 * piece), 2 * piece), 2 * piece)

    def unit_chip(i):
        return jnp.where(chip < n_chip // 2, turns - i, i)

    last_depth = depth // blocks
    early = depth - last_depth

    def unit(layer, some, h, i):

        @pl.when(i == 0)
        def _():
            @pl.when(h + 1 < PARTS)
            def _():
                relay(layer, some, h + 1)

            @pl.when(h + 3 < PARTS)
            def _():
                near_start(layer, some, h + 3)

            arrive(layer, some, h)

        d = unit_chip(i)
        if layer == 0 or blocks == 1:
            value = jnp.dot(
                dense[chip_rows(d), :], inputs[layer, h], preferred_element_type=jnp.float32
            )
            prod[layer, h, d] = value.reshape(2, piece, part)
        else:
            value = jnp.dot(
                dense[chip_rows(d), early:], inputs[layer, h, early:, :],
                preferred_element_type=jnp.float32,
            )
            prod[layer, h, d] += value.reshape(2, piece, part)
        pair_copy(layer, h, d).start()

    def early_unit(i):
        d = unit_chip(i)
        known = jnp.concatenate([inputs[1, h, 0:early, :] for h in range(PARTS)], axis=1)
        value = jnp.dot(dense[chip_rows(d), 0:early], known, preferred_element_type=jnp.float32)
        for h in range(PARTS):
            prod[1, h, d] = value[:, h * part : (h + 1) * part].reshape(2, piece, part)

    everything = list(range(blocks))
    units = PARTS * turns
    settle_time = max(units, LEAD + turns * (PARTS - 1) + SKEW * turns + 1)
    end_time = LEAD + steps + SKEW * (turns - 1)
    relay_time = settle_time + 2
    relay_end = relay_time + PARTS

    def run(layer, some, begin, end, extra=None):
        def body(u, carry):
            send_step(layer, u - LEAD)
            if begin < units:
                @pl.when(u < units)
                def _():
                    h, i = u // turns, lax.rem(u, turns)
                    extra_unit = jnp.where(i == turns - 1, 1, 0)

                    def one(n, inner):
                        unit(layer, some, h, i + n)
                        return inner

                    lax.fori_loop(0, 1 + extra_unit, one, 0)

            if extra is not None:
                extra(u - begin)
            return carry

        lax.fori_loop(begin, end, body, 0)

    def hide(b):
        value = jnp.maximum(project(0, b), 0.0).astype(inputs.dtype)
        for h in range(PARTS):
            inputs[1, h, slot_rows(b, row), :] = value[:, h * part : (h + 1) * part]

    def gather_begin(layer, some):
        near_start(layer, some, 0)
        if PARTS > 1:
            near_start(layer, some, 1)

    def gather_next(layer, some):
        relay(layer, some, 0)
        if PARTS > 2:
            near_start(layer, some, 2)

    def early_relay(h):
        relay(1, [0], h)

        @pl.when(h + 2 < PARTS)
        def _():
            near_start(1, [0], h + 2)

    def drain(layer):
        for h in range(PARTS):
            for b in range(blocks):
                for i in range(len(bits)):
                    near_copy(layer, b, h, i).wait_send()
                for i in range(len(masks)):
                    for side in (0, 1):
                        far_copy(layer, b, h, i, side).wait_send()

            def drain_pair(d, carry):
                pair_copy(layer, h, d).wait_send()
                return carry

            lax.fori_loop(0, n_chip, drain_pair, 0)

        def drain_flow(k, carry):
            b, h, j = place_of(k)
            for way in (0, 1):
                d = turns - j if way == 0 else j
                ahead = d > chip if way == 0 else d < chip

                @pl.when(ahead)
                def _():
                    flow_copy(layer, way, k).wait_send()
                    if LINK_TYPES[layer] == jnp.int16:
                        scale_copy(way, k).wait_send()

            return carry

        lax.fori_loop(0, steps, drain_flow, 0)

    def out_copy(b):
        rows = pl.ds(b * sub, sub)
        return pltpu.make_async_copy(result.at[rows, :], out_hbm.at[rows, :], out_sem.at[b])

    for loads in feature_loads:
        for load in loads:
            load.wait()
    pl.semaphore_wait(barrier, peers)
    gather_begin(0, everything)

    tiles[slots] = jnp.zeros((tile, tile), tiles.dtype)
    spots = tile_rows * tile_cols
    counts_load.wait()
    places_load.wait()
    count = counts[row, col]
    order = lax.broadcasted_iota(jnp.int32, (spots, slots), 1)
    spot = lax.broadcasted_iota(jnp.int32, (spots, slots), 0)
    place = places[0:1, :] * tile_cols + places[1:2, :]
    listed = (place == spot) & (order < count)
    marks = jnp.where(listed, order - slots, 0)
    found = jnp.sum(marks.T, axis=0, keepdims=True) + slots
    inverse_rows[...] = jnp.broadcast_to(found, inverse_rows.shape)
    inverse_load = pltpu.make_async_copy(inverse_rows, inverse_ref, load_sem.at[3])
    inverse_load.start()
    inverse_load.wait()
    tile_load.wait()

    def place_row(i, carry):
        rows = pl.ds(pl.multiple_of(i * tile, tile), tile)
        for t in range(tile_cols):
            at = (t % blocks) * (tile_cols // blocks) + t // blocks
            slot = jnp.clip(inverse_ref[0, i * tile_cols + t], 0, slots)
            dense[rows, at * tile : (at + 1) * tile] = tiles[slot]
        return carry

    lax.fori_loop(0, tile_rows, place_row, 0)
    gather_next(0, everything)
    for load in weight_loads:
        load.wait()

    if blocks == 1:
        run(0, everything, 0, end_time)
    else:
        run(0, everything, 0, settle_time)
        settle(0, 0)
        hide(0)
        gather_begin(1, [0])
        run(0, everything, settle_time, relay_time)
        run(0, everything, relay_time, relay_end, early_relay)
        run(0, everything, relay_end, max(relay_end, end_time))
    settle(0, blocks - 1)
    hide(blocks - 1)
    late = [blocks - 1]
    gather_begin(1, late)
    if blocks > 1:
        for h in range(PARTS):
            arrive(1, [0], h)
        early_unit(0)
        early_unit(1)
        gather_next(1, late)
        for i in range(2, n_chip):
            early_unit(i)
    else:
        gather_next(1, late)
    if blocks == 1:
        run(1, late, 0, end_time)
    else:
        run(1, late, 0, settle_time)
        settle(1, 0)
        result[0:sub, :] = project(1, 0)
        out_copy(0).start()
        run(1, late, settle_time, end_time)
    drain(0)
    drain(1)
    settle(1, blocks - 1)
    result[(blocks - 1) * sub :, :] = project(1, blocks - 1)
    out_copy(blocks - 1).start()
    for b in range(blocks):
        out_copy(b).wait()


def shards(n_row, n_col, features, tile_values, tile_places, tile_counts, weight_one, weight_two):
    tiles = tile_values.reshape(tile_values.shape[2:])
    places = tile_places.reshape(tile_places.shape[2:])
    slots, tile = tiles.shape[0], tiles.shape[1]
    piece, width = features.shape
    part = width // PARTS
    blocks = 2 if piece == 2 * tile else 1
    sub = piece // blocks
    rows, depth = piece * n_col, piece * n_row
    tile_rows, tile_cols = rows // tile, depth // tile
    n_chip = n_col // 2
    spots = tile_rows * tile_cols
    steps = blocks * PARTS * (n_chip - 1)
    n_bits = (n_row - 1).bit_length()
    n_far = max(1, n_row - 1 - n_bits)

    def flow(layer):
        return pltpu.VMEM((steps, sub, part), LINK_TYPES[layer])

    dma = pltpu.SemaphoreType.DMA
    any_space = pl.BlockSpec(memory_space=pl.ANY)
    second = pl.pallas_call(
        functools.partial(kernel, n_row, n_col, blocks),
        out_shape=jax.ShapeDtypeStruct((piece, width), jnp.float32),
        in_specs=[any_space] * 6,
        out_specs=any_space,
        scratch_shapes=[
            pltpu.VMEM((slots + 1, tile, tile), jnp.bfloat16),
            pltpu.VMEM((rows, depth), jnp.bfloat16),
            pltpu.VMEM((2, width, width), jnp.float32),
            pltpu.VMEM((2, PARTS, depth, part), jnp.bfloat16),
            pltpu.VMEM((blocks, sub, width), jnp.float32),
            pltpu.VMEM((piece, width), jnp.float32),
            pltpu.VMEM((2, PARTS, n_chip, 2, piece, part), jnp.float32),
            pltpu.VMEM((2, PARTS, n_chip, piece, part), jnp.float32),
            flow(0), flow(0), flow(0), flow(0), flow(1), flow(1), flow(1), flow(1),
            pltpu.VMEM((2, steps, 1, part), jnp.float32),
            pltpu.VMEM((2, steps, 1, part), jnp.float32),
            dma((6,)), dma((blocks, PARTS)), dma((blocks,)),
            dma((2, blocks, PARTS, n_bits)), dma((2, blocks, PARTS, n_bits)),
            dma((2, blocks, PARTS, n_far, 2)), dma((2, blocks, PARTS, n_far, 2)),
            dma((2, PARTS, n_chip)), dma((2, PARTS, n_chip)),
            dma((2, 2, steps)), dma((2, 2, steps)),
            dma((2, steps)), dma((2, steps)),
            pltpu.SMEM(tile_counts.shape, jnp.int32), pltpu.VMEM(places.shape, jnp.int32),
            pltpu.VMEM((8, spots), jnp.int32), pltpu.SMEM((8, spots), jnp.int32),
        ],
        compiler_params=pltpu.CompilerParams(
            collective_id=0, has_side_effects=True, vmem_limit_bytes=60 * 1024 * 1024
        ),
    )(tile_counts, places, features, tiles, weight_one, weight_two)
    return jnp.maximum(second, 0.0)


def solution(mesh):
    placed = (
        P(("row", "col"), None),
        P("row", "col", None, None, None),
        P("row", "col", None, None),
        P(),
        P(),
        P(),
    )
    return jax.shard_map(
        functools.partial(shards, mesh.shape["row"], mesh.shape["col"]),
        mesh=mesh, in_specs=placed, out_specs=P(("row", "col"), None), check_vma=False,
    )
```

time: 76.6 us -> 77.2 us (level)
  no operation moved by 1% of the time
where the time goes in v1:
time: 77.2 us; the launch traced here: 77 us
  Pallas kernels  75.2 us (97%)
  other arithmetic  1.88 us (2%)
    pallas_call x1, Pallas kernels, shards(): pl.pallas_call(functools.partial(kernel, n_row, n_col, blocks), out_shape...  75.2 us
    max x1, other arithmetic, shards(): return jnp.maximum(second, 0.0)  1.88 us

profile of v1, /device:TPU:0, one launch (start us, length us, event | category | flops | bytes accessed | tf_op | source)
XLA Modules:
  0.0 77.0 jit_solution(3654368298484249216)
XLA Ops:
  0.0 75.2 %shard_map.64 = f32[256,512]{1,0:T(8,128)} custom-call(s32[4,8]{1,0:T(4,128)} %counts_hbm.1, s32[2,128]{1,0:T(2,128)} %bitcast.3, bf16[256,512]{1,0:T(8,128)(2,1)} %features_hbm.1, bf16[128,128,128]{2,1,0:T(8,128)(2,1)} %bitcast.2, f32[512,512]{1,0:T(8,128)} %weight_one_hbm.1, f32[512,512]{1,0:T(8,128)} %weight_two_hbm.1), custom_call_target="tpu_custom_call" | custom-call | tf_op jit(solution)/shard_map/pallas_call | solution.py:477
  75.2 1.9 %broadcast_maximum_fusion = f32[256,512]{1,0:T(8,128)} fusion(f32[256,512]{1,0:T(8,128)} %shard_map.64), kind=kLoop, calls=%fused_computation | loop fusion | flops 131072 | bytes 1048576 | tf_op jit(solution)/shard_map/max | solution.py:507

commit v2 on v0

v2 whole, which is shorter than its diff:
```python
import functools

import jax
import jax.numpy as jnp
from jax import lax
from jax.experimental import pallas as pl
from jax.experimental.pallas import tpu as pltpu
from jax.sharding import PartitionSpec as P

MESH = pl.DeviceIdType.MESH
PARTS = 4
LINK_TYPES = (jnp.int16, jnp.bfloat16)
TOP = 32766.0
LEAD = 2


def kernel(
    n_row, n_col, blocks,
    counts_hbm, places_hbm, features_hbm, tiles_hbm, weight_one_hbm, weight_two_hbm,
    out_hbm,
    tiles, dense, weights, inputs, total, result, prod, pair_in,
    out0, out1, land0, land1, via0, via1, scale_out, scale_land, scale_via,
    load_sem, feature_sem, out_sem, gather_send, gather_recv, pair_send, pair_recv,
    link_send, land_recv, via_recv, scale_send, scale_land_recv, scale_via_recv,
    counts, places, inverse_rows, inverse_ref,
):
    row, col = lax.axis_index("row"), lax.axis_index("col")
    n_chip = n_col // 2
    chip, core = col // 2, col % 2
    partner = chip * 2 + (1 - core)
    slots, tile = tiles_hbm.shape[0], tiles_hbm.shape[1]
    piece, width = features_hbm.shape
    part = width // PARTS
    sub = piece // blocks
    depth = piece * n_row
    tile_rows, tile_cols = dense.shape[0] // tile, depth // tile
    turns = n_chip - 1

    barrier = pltpu.get_barrier_semaphore()

    def greet(step, carry):
        pl.semaphore_signal(
            barrier, inc=1, device_id=(row, lax.rem(chip + step, n_chip) * 2 + core),
            device_id_type=MESH,
        )
        return carry

    lax.fori_loop(1, n_chip, greet, 0)
    for step in range(1, n_row):
        pl.semaphore_signal(
            barrier, inc=1, device_id=(lax.rem(row + step, n_row), col), device_id_type=MESH
        )
    pl.semaphore_signal(barrier, inc=1, device_id=(row, partner), device_id_type=MESH)

    def slot_rows(b, q):
        return pl.ds(pl.multiple_of((b * n_row + q) * sub, sub), sub)

    feature_loads = [
        [
            pltpu.make_async_copy(
                features_hbm.at[pl.ds(b * sub, sub), pl.ds(h * part, part)],
                inputs.at[0, h, slot_rows(b, row), :],
                feature_sem.at[b, h],
            )
            for b in range(blocks)
        ]
        for h in range(PARTS)
    ]
    for loads in feature_loads:
        for load in loads:
            load.start()
    peers = n_row - 1 + 1 + n_chip - 1
    end_chip = (chip == 0) | (chip == turns)
    neighbour = jnp.where(chip == 0, 1, turns - 1)

    def gather_copy(layer, b, h, step):
        block = inputs.at[layer, h, slot_rows(b, row), :]
        return pltpu.make_async_remote_copy(
            src_ref=block, dst_ref=block,
            send_sem=gather_send.at[layer, b, h, step - 1],
            recv_sem=gather_recv.at[layer, b, h, step - 1],
            device_id=(lax.rem(row + step, n_row), col), device_id_type=MESH,
        )

    def gather_start(layer, b, h):
        for step in range(1, n_row):
            gather_copy(layer, b, h, step).start()

    def gather_wait(layer, b, h):
        for step in range(1, n_row):
            gather_copy(layer, b, h, step).wait_recv()

    def pair_copy(layer, h, d):
        return pltpu.make_async_remote_copy(
            src_ref=prod.at[layer, h, d, 1 - core],
            dst_ref=pair_in.at[layer, h, d],
            send_sem=pair_send.at[layer, h, d], recv_sem=pair_recv.at[layer, h, d],
            device_id=(row, partner), device_id_type=MESH,
        )

    outs, lands, vias = (out0, out1), (land0, land1), (via0, via1)

    def spot_of(b, h, d):
        return (b * PARTS + h) * n_chip + d

    def link_copy(layer, b, h, d, target, scale, via):
        at, here = spot_of(b, h, d), spot_of(b, h, chip)
        if via:
            there = spot_of(b - 1, h, d)
            place = (scale_via if scale else vias[layer]).at[there]
            recv = (scale_via_recv if scale else via_recv.at[layer]).at[there]
        else:
            place = (scale_land if scale else lands[layer]).at[here]
            recv = (scale_land_recv if scale else land_recv.at[layer]).at[here]
        return pltpu.make_async_remote_copy(
            src_ref=(scale_out if scale else outs[layer]).at[at], dst_ref=place,
            send_sem=(scale_send if scale else link_send.at[layer]).at[at], recv_sem=recv,
            device_id=(row, target * 2 + core), device_id_type=MESH,
        )

    def both(layer):
        return (True, False) if LINK_TYPES[layer] == jnp.int16 else (False,)

    def post(layer, b, h, d, value):
        at = spot_of(b, h, d)
        if LINK_TYPES[layer] == jnp.int16:
            peak = jnp.maximum(jnp.max(jnp.abs(value), axis=0, keepdims=True), 1e-30)
            scale_out[at] = peak * (1.0 / TOP)
            outs[layer][at] = jnp.round(value * (TOP / peak)).astype(jnp.int32).astype(jnp.int16)
        else:
            outs[layer][at] = value.astype(outs[layer].dtype)
        if b == 0:
            for scale in both(layer):
                link_copy(layer, b, h, d, d, scale, False).start()
        else:
            detour = end_chip & (d != neighbour)

            @pl.when(detour)
            def _():
                for scale in both(layer):
                    link_copy(layer, b, h, d, neighbour, scale, True).start()

            @pl.when(jnp.logical_not(detour))
            def _():
                for scale in both(layer):
                    link_copy(layer, b, h, d, d, scale, False).start()

    def decode(layer, block, scale):
        if LINK_TYPES[layer] == jnp.int16:
            return block.astype(jnp.int32).astype(jnp.float32) * scale
        return block.astype(jnp.float32)

    def take_land(layer, b, h, s):
        at = spot_of(b, h, s)
        for scale in both(layer):
            pltpu.make_async_remote_copy(
                src_ref=(scale_out if scale else outs[layer]).at[at],
                dst_ref=(scale_land if scale else lands[layer]).at[at],
                send_sem=(scale_send if scale else link_send.at[layer]).at[at],
                recv_sem=(scale_land_recv if scale else land_recv.at[layer]).at[at],
                device_id=(row, partner), device_id_type=MESH,
            ).wait_recv()
        return decode(layer, lands[layer][at], scale_land[at])

    def take_via(layer, b, h, d):
        at = spot_of(b - 1, h, d)
        for scale in both(layer):
            link_copy(layer, b, h, d, partner // 2, scale, True).wait_recv()
        return decode(layer, vias[layer][at], scale_via[at])

    def pair_sum(layer, b, h, d):
        rows = pl.ds(b * sub, sub)
        return prod[layer, h, d, core, rows, :] + pair_in[layer, h, d, rows, :]

    def send(layer, b, h, d):
        if b == 0:
            post(layer, b, h, d, pair_sum(layer, b, h, d))
        else:
            merged = ((chip == 1) & (d > 1)) | ((chip == turns - 1) & (d < turns - 1))

            @pl.when(merged)
            def _():
                post(layer, b, h, d, pair_sum(layer, b, h, d) + take_via(layer, b, h, d))

            @pl.when(jnp.logical_not(merged))
            def _():
                post(layer, b, h, d, pair_sum(layer, b, h, d))

    def sources(b, s):
        if b == 0:
            return s != chip
        first_hop = ((s == 0) & (chip != 1)) | ((s == turns) & (chip != turns - 1))
        return (s != chip) & jnp.logical_not(first_hop)

    def settle(layer, b):
        for h in range(PARTS):
            columns = slice(h * part, (h + 1) * part)
            total[b, :, columns] = pair_sum(layer, b, h, chip)

            def add(s, carry):
                @pl.when(sources(b, s))
                def _():
                    total[b, :, columns] += take_land(layer, b, h, s)

                return carry

            lax.fori_loop(0, n_chip, add, 0)

    def project(layer, b):
        return jnp.dot(
            total[b], weights[layer], precision=lax.Precision.HIGHEST,
            preferred_element_type=jnp.float32,
        )

    def chip_rows(d):
        return pl.ds(pl.multiple_of(d * (2 * piece), 2 * piece), 2 * piece)

    def unit_chip(i):
        return jnp.where(chip < n_chip // 2, turns - i, i)

    def late_chip(i):
        return jnp.where(
            chip < n_chip // 2, lax.rem(n_chip - i, n_chip), lax.rem(turns + i, n_chip)
        )

    early = depth - depth // blocks
    known_parts = PARTS - 1

    def unit(layer, u):
        h, i = u // n_chip, lax.rem(u, n_chip)
        split = layer == 1 and blocks > 1

        @pl.when(i == 0)
        def _():
            if split:
                @pl.when(h >= known_parts)
                def _():
                    gather_wait(layer, 0, h)

                gather_wait(layer, 1, h)
            else:
                for b in range(blocks):
                    gather_wait(layer, b, h)

        d = unit_chip(i)

        def whole():
            value = jnp.dot(
                dense[chip_rows(d), :], inputs[layer, h], preferred_element_type=jnp.float32
            )
            prod[layer, h, d] = value.reshape(2, piece, part)

        if split:
            @pl.when(h < known_parts)
            def _():
                value = jnp.dot(
                    dense[chip_rows(d), early:], inputs[layer, h, early:, :],
                    preferred_element_type=jnp.float32,
                )
                prod[layer, h, d] += value.reshape(2, piece, part)

            @pl.when(h >= known_parts)
            def _():
                whole()
        else:
            whole()
        pair_copy(layer, h, d).start()

    def early_unit(i):
        d = unit_chip(i)
        known = jnp.concatenate([inputs[1, h, 0:early, :] for h in range(known_parts)], axis=1)
        value = jnp.dot(dense[chip_rows(d), 0:early], known, preferred_element_type=jnp.float32)
        for h in range(known_parts):
            prod[1, h, d] = value[:, h * part : (h + 1) * part].reshape(2, piece, part)

    units = PARTS * n_chip

    def run_first(layer):
        def body(u, carry):
            k = u - LEAD

            @pl.when(k >= 0)
            def _():
                h, d = k // n_chip, unit_chip(lax.rem(k, n_chip))
                pair_copy(layer, h, d).wait_recv()

                @pl.when(d != chip)
                def _():
                    send(layer, 0, h, d)

                @pl.when((d != chip) & end_chip & (h == 0))
                def _():
                    for b in range(1, blocks):
                        send(layer, b, h, d)

            @pl.when(u < units)
            def _():
                unit(layer, u)

            return carry

        lax.fori_loop(0, units + LEAD, body, 0)

    def run_rest(layer, begin, end):
        def body(w, carry):
            d, h = late_chip(w // PARTS), lax.rem(w, PARTS)

            @pl.when((d != chip) & jnp.logical_not(end_chip & (h == 0)))
            def _():
                for b in range(1, blocks):
                    send(layer, b, h, d)

            return carry

        if blocks > 1:
            lax.fori_loop(begin, end, body, 0)

    def hide(b):
        value = jnp.maximum(project(0, b), 0.0).astype(inputs.dtype)
        for h in range(PARTS):
            inputs[1, h, slot_rows(b, row), :] = value[:, h * part : (h + 1) * part]

    def drain(layer):
        for h in range(PARTS):
            for b in range(blocks):
                for step in range(1, n_row):
                    gather_copy(layer, b, h, step).wait_send()

        def drain_pair(d, carry):
            for h in range(PARTS):
                pair_copy(layer, h, d).wait_send()

                @pl.when(d != chip)
                def _():
                    for b in range(blocks):
                        for scale in both(layer):
                            link_copy(layer, b, h, d, d, scale, False).wait_send()

            return carry

        lax.fori_loop(0, n_chip, drain_pair, 0)

    def out_copy(b):
        rows = pl.ds(b * sub, sub)
        return pltpu.make_async_copy(result.at[rows, :], out_hbm.at[rows, :], out_sem.at[b])

    for loads in feature_loads:
        for load in loads:
            load.wait()
    counts_load = pltpu.make_async_copy(counts_hbm, counts, load_sem.at[4])
    counts_load.start()
    places_load = pltpu.make_async_copy(places_hbm, places, load_sem.at[5])
    places_load.start()
    tile_load = pltpu.make_async_copy(tiles_hbm, tiles.at[pl.ds(0, slots)], load_sem.at[0])
    tile_load.start()
    weight_loads = [
        pltpu.make_async_copy(weight_one_hbm, weights.at[0], load_sem.at[1]),
        pltpu.make_async_copy(weight_two_hbm, weights.at[1], load_sem.at[2]),
    ]
    for load in weight_loads:
        load.start()

    pl.semaphore_wait(barrier, peers)
    for h in range(PARTS):
        for b in range(blocks):
            gather_start(0, b, h)

    tiles[slots] = jnp.zeros((tile, tile), tiles.dtype)
    spots = tile_rows * tile_cols
    counts_load.wait()
    places_load.wait()
    count = counts[row, col]
    order = lax.broadcasted_iota(jnp.int32, (spots, slots), 1)
    spot = lax.broadcasted_iota(jnp.int32, (spots, slots), 0)
    place = places[0:1, :] * tile_cols + places[1:2, :]
    listed = (place == spot) & (order < count)
    marks = jnp.where(listed, order - slots, 0)
    found = jnp.sum(marks.T, axis=0, keepdims=True) + slots
    inverse_rows[...] = jnp.broadcast_to(found, inverse_rows.shape)
    inverse_load = pltpu.make_async_copy(inverse_rows, inverse_ref, load_sem.at[3])
    inverse_load.start()
    inverse_load.wait()
    tile_load.wait()

    def place_row(i, carry):
        rows = pl.ds(pl.multiple_of(i * tile, tile), tile)
        for t in range(tile_cols):
            at = (t % blocks) * (tile_cols // blocks) + t // blocks
            slot = jnp.clip(inverse_ref[0, i * tile_cols + t], 0, slots)
            dense[rows, at * tile : (at + 1) * tile] = tiles[slot]
        return carry

    lax.fori_loop(0, tile_rows, place_row, 0)
    for load in weight_loads:
        load.wait()

    middle = jnp.where(end_chip, units, units // 2)
    run_first(0)
    run_rest(0, 0, middle)
    if blocks > 1:
        settle(0, 0)
        hide(0)
        for h in range(known_parts):
            gather_start(1, 0, h)
    run_rest(0, middle, units)
    settle(0, blocks - 1)
    hide(blocks - 1)
    gather_start(1, blocks - 1, 0)
    if blocks > 1:
        for h in range(known_parts, PARTS):
            gather_start(1, 0, h)
    for h in range(1, PARTS):
        gather_start(1, blocks - 1, h)
    if blocks > 1:
        for h in range(known_parts):
            gather_wait(1, 0, h)
        for i in range(n_chip):
            early_unit(i)
    run_first(1)
    run_rest(1, 0, middle)
    drain(0)
    if blocks > 1:
        settle(1, 0)
        result[0:sub, :] = project(1, 0)
        out_copy(0).start()
    run_rest(1, middle, units)
    drain(1)
    settle(1, blocks - 1)
    result[(blocks - 1) * sub :, :] = project(1, blocks - 1)
    out_copy(blocks - 1).start()
    for b in range(blocks):
        out_copy(b).wait()


def shards(n_row, n_col, features, tile_values, tile_places, tile_counts, weight_one, weight_two):
    tiles = tile_values.reshape(tile_values.shape[2:])
    places = tile_places.reshape(tile_places.shape[2:])
    slots, tile = tiles.shape[0], tiles.shape[1]
    piece, width = features.shape
    part = width // PARTS
    blocks = 2 if piece == 2 * tile else 1
    sub = piece // blocks
    rows, depth = piece * n_col, piece * n_row
    tile_rows, tile_cols = rows // tile, depth // tile
    n_chip = n_col // 2
    spots = tile_rows * tile_cols
    items = blocks * PARTS * n_chip
    detours = max(1, (blocks - 1) * PARTS * n_chip)

    def flow(layer, count):
        return pltpu.VMEM((count, sub, part), LINK_TYPES[layer])

    def scales(count):
        return pltpu.VMEM((count, 1, part), jnp.float32)

    dma = pltpu.SemaphoreType.DMA
    any_space = pl.BlockSpec(memory_space=pl.ANY)
    second = pl.pallas_call(
        functools.partial(kernel, n_row, n_col, blocks),
        out_shape=jax.ShapeDtypeStruct((piece, width), jnp.float32),
        in_specs=[any_space] * 6,
        out_specs=any_space,
        scratch_shapes=[
            pltpu.VMEM((slots + 1, tile, tile), jnp.bfloat16),
            pltpu.VMEM((rows, depth), jnp.bfloat16),
            pltpu.VMEM((2, width, width), jnp.float32),
            pltpu.VMEM((2, PARTS, depth, part), jnp.bfloat16),
            pltpu.VMEM((blocks, sub, width), jnp.float32),
            pltpu.VMEM((piece, width), jnp.float32),
            pltpu.VMEM((2, PARTS, n_chip, 2, piece, part), jnp.float32),
            pltpu.VMEM((2, PARTS, n_chip, piece, part), jnp.float32),
            flow(0, items), flow(1, items), flow(0, items), flow(1, items),
            flow(0, detours), flow(1, detours),
            scales(items), scales(items), scales(detours),
            dma((6,)), dma((blocks, PARTS)), dma((blocks,)),
            dma((2, blocks, PARTS, n_row - 1)), dma((2, blocks, PARTS, n_row - 1)),
            dma((2, PARTS, n_chip)), dma((2, PARTS, n_chip)),
            dma((2, items)), dma((2, items)), dma((2, detours)),
            dma((items,)), dma((items,)), dma((detours,)),
            pltpu.SMEM(tile_counts.shape, jnp.int32), pltpu.VMEM(places.shape, jnp.int32),
            pltpu.VMEM((8, spots), jnp.int32), pltpu.SMEM((8, spots), jnp.int32),
        ],
        compiler_params=pltpu.CompilerParams(
            collective_id=0, has_side_effects=True, vmem_limit_bytes=60 * 1024 * 1024
        ),
    )(tile_counts, places, features, tiles, weight_one, weight_two)
    return jnp.maximum(second, 0.0)


def solution(mesh):
    placed = (
        P(("row", "col"), None),
        P("row", "col", None, None, None),
        P("row", "col", None, None),
        P(),
        P(),
        P(),
    )
    return jax.shard_map(
        functools.partial(shards, mesh.shape["row"], mesh.shape["col"]),
        mesh=mesh, in_specs=placed, out_specs=P(("row", "col"), None), check_vma=False,
    )
```

time: 76.6 us -> 67.4 us (0.88)
  Pallas kernels: 74.5 us -> 65.3 us
    pallas_call x1, Pallas kernels: 74.5 us -> 65.3 us  [shards(): pl.pallas_call(functools.partial(kernel, n_row, n_col, blocks), out_shape...]
where the time goes in v2:
time: 67.4 us; the launch traced here: 67.2 us
  Pallas kernels  65.3 us (97%)
  other arithmetic  1.88 us (3%)
    pallas_call x1, Pallas kernels, shards(): pl.pallas_call(functools.partial(kernel, n_row, n_col, blocks), out_shape...  65.3 us
    max x1, other arithmetic, shards(): return jnp.maximum(second, 0.0)  1.88 us

profile of v2, /device:TPU:0, one launch (start us, length us, event | category | flops | bytes accessed | tf_op | source)
XLA Modules:
  0.0 67.2 jit_solution(1754276868034944807)
XLA Ops:
  0.0 65.3 %shard_map.64 = f32[256,512]{1,0:T(8,128)} custom-call(s32[4,8]{1,0:T(4,128)} %counts_hbm.1, s32[2,128]{1,0:T(2,128)} %bitcast.3, bf16[256,512]{1,0:T(8,128)(2,1)} %features_hbm.1, bf16[128,128,128]{2,1,0:T(8,128)(2,1)} %bitcast.2, f32[512,512]{1,0:T(8,128)} %weight_one_hbm.1, f32[512,512]{1,0:T(8,128)} %weight_two_hbm.1), custom_call_target="tpu_custom_call" | custom-call | tf_op jit(solution)/shard_map/pallas_call | solution.py:458
  65.3 1.9 %broadcast_maximum_fusion = f32[256,512]{1,0:T(8,128)} fusion(f32[256,512]{1,0:T(8,128)} %shard_map.64), kind=kLoop, calls=%fused_computation | loop fusion | flops 131072 | bytes 1048576 | tf_op jit(solution)/shard_map/max | solution.py:487

commit v3 on v2

--- a/solution.py
+++ b/solution.py
@@ -11,7 +11,7 @@
 PARTS = 4
 LINK_TYPES = (jnp.int16, jnp.bfloat16)
 TOP = 32766.0
-LEAD = 2
+LEAD = 3
 
 
 def kernel(
@@ -60,7 +60,7 @@
             pltpu.make_async_copy(
                 features_hbm.at[pl.ds(b * sub, sub), pl.ds(h * part, part)],
                 inputs.at[0, h, slot_rows(b, row), :],
-                feature_sem.at[b, h],
+                feature_sem,
             )
             for b in range(blocks)
         ]
@@ -77,8 +77,7 @@
         block = inputs.at[layer, h, slot_rows(b, row), :]
         return pltpu.make_async_remote_copy(
             src_ref=block, dst_ref=block,
-            send_sem=gather_send.at[layer, b, h, step - 1],
-            recv_sem=gather_recv.at[layer, b, h, step - 1],
+            send_sem=gather_send.at[layer], recv_sem=gather_recv.at[layer, b, h],
             device_id=(lax.rem(row + step, n_row), col), device_id_type=MESH,
         )
 
@@ -86,15 +85,21 @@
         for step in range(1, n_row):
             gather_copy(layer, b, h, step).start()
 
+    def whole_wait(block, send_sem, recv_sem):
+        return pltpu.make_async_remote_copy(
+            src_ref=block, dst_ref=block, send_sem=send_sem, recv_sem=recv_sem,
+            device_id=(row, partner), device_id_type=MESH,
+        )
+
     def gather_wait(layer, b, h):
-        for step in range(1, n_row):
-            gather_copy(layer, b, h, step).wait_recv()
+        block = inputs.at[layer, h, pl.ds(0, (n_row - 1) * sub), :]
+        whole_wait(block, gather_send.at[layer], gather_recv.at[layer, b, h]).wait_recv()
 
     def pair_copy(layer, h, d):
         return pltpu.make_async_remote_copy(
             src_ref=prod.at[layer, h, d, 1 - core],
             dst_ref=pair_in.at[layer, h, d],
-            send_sem=pair_send.at[layer, h, d], recv_sem=pair_recv.at[layer, h, d],
+            send_sem=pair_send.at[layer], recv_sem=pair_recv.at[layer, h, d],
             device_id=(row, partner), device_id_type=MESH,
         )
 
@@ -111,10 +116,10 @@
             recv = (scale_via_recv if scale else via_recv.at[layer]).at[there]
         else:
             place = (scale_land if scale else lands[layer]).at[here]
-            recv = (scale_land_recv if scale else land_recv.at[layer]).at[here]
+            recv = (scale_land_recv if scale else land_recv.at[layer]).at[b, chip]
         return pltpu.make_async_remote_copy(
             src_ref=(scale_out if scale else outs[layer]).at[at], dst_ref=place,
-            send_sem=(scale_send if scale else link_send.at[layer]).at[at], recv_sem=recv,
+            send_sem=scale_send if scale else link_send.at[layer], recv_sem=recv,
             device_id=(row, target * 2 + core), device_id_type=MESH,
         )
 
@@ -150,16 +155,16 @@
             return block.astype(jnp.int32).astype(jnp.float32) * scale
         return block.astype(jnp.float32)
 
+    def land_wait(layer, b, s):
+        for scale in both(layer):
+            whole_wait(
+                (scale_land if scale else lands[layer]).at[pl.ds(0, PARTS)],
+                scale_send if scale else link_send.at[layer],
+                (scale_land_recv if scale else land_recv.at[layer]).at[b, s],
+            ).wait_recv()
+
     def take_land(layer, b, h, s):
         at = spot_of(b, h, s)
-        for scale in both(layer):
-            pltpu.make_async_remote_copy(
-                src_ref=(scale_out if scale else outs[layer]).at[at],
-                dst_ref=(scale_land if scale else lands[layer]).at[at],
-                send_sem=(scale_send if scale else link_send.at[layer]).at[at],
-                recv_sem=(scale_land_recv if scale else land_recv.at[layer]).at[at],
-                device_id=(row, partner), device_id_type=MESH,
-            ).wait_recv()
         return decode(layer, lands[layer][at], scale_land[at])
 
     def take_via(layer, b, h, d):
@@ -194,17 +199,20 @@
 
     def settle(layer, b):
         for h in range(PARTS):
-            columns = slice(h * part, (h + 1) * part)
-            total[b, :, columns] = pair_sum(layer, b, h, chip)
-
-            def add(s, carry):
-                @pl.when(sources(b, s))
-                def _():
-                    total[b, :, columns] += take_land(layer, b, h, s)
-
-                return carry
-
-            lax.fori_loop(0, n_chip, add, 0)
+            total[b, :, h * part : (h + 1) * part] = pair_sum(layer, b, h, chip)
+
+        def add(i, carry):
+            s = late_chip(i)
+
+            @pl.when(sources(b, s))
+            def _():
+                land_wait(layer, b, s)
+                for h in range(PARTS):
+                    total[b, :, h * part : (h + 1) * part] += take_land(layer, b, h, s)
+
+            return carry
+
+        lax.fori_loop(0, n_chip, add, 0)
 
     def project(layer, b):
         return jnp.dot(
@@ -242,6 +250,18 @@
                 for b in range(blocks):
                     gather_wait(layer, b, h)
 
+            @pl.when(h + 2 < PARTS)
+            def _():
+                if split:
+                    @pl.when(h + 2 >= known_parts)
+                    def _():
+                        gather_start(layer, 0, h + 2)
+
+                    gather_start(layer, 1, h + 2)
+                else:
+                    for b in range(blocks):
+                        gather_start(layer, b, h + 2)
+
         d = unit_chip(i)
 
         def whole():
@@ -321,32 +341,24 @@
             inputs[1, h, slot_rows(b, row), :] = value[:, h * part : (h + 1) * part]
 
     def drain(layer):
-        for h in range(PARTS):
-            for b in range(blocks):
-                for step in range(1, n_row):
-                    gather_copy(layer, b, h, step).wait_send()
-
-        def drain_pair(d, carry):
-            for h in range(PARTS):
-                pair_copy(layer, h, d).wait_send()
-
-                @pl.when(d != chip)
-                def _():
-                    for b in range(blocks):
-                        for scale in both(layer):
-                            link_copy(layer, b, h, d, d, scale, False).wait_send()
-
-            return carry
-
-        lax.fori_loop(0, n_chip, drain_pair, 0)
+        sent = inputs.at[layer, :, pl.ds(0, depth // n_row * (n_row - 1)), :]
+        whole_wait(sent, gather_send.at[layer], gather_recv.at[layer, 0, 0]).wait_send()
+        whole_wait(
+            pair_in.at[layer], pair_send.at[layer], pair_recv.at[layer, 0, 0]
+        ).wait_send()
+        for scale in both(layer):
+            whole_wait(
+                (scale_out if scale else outs[layer]).at[pl.ds(0, blocks * PARTS * turns)],
+                scale_send if scale else link_send.at[layer],
+                (scale_land_recv if scale else land_recv.at[layer]).at[0, 0],
+            ).wait_send()
 
     def out_copy(b):
         rows = pl.ds(b * sub, sub)
         return pltpu.make_async_copy(result.at[rows, :], out_hbm.at[rows, :], out_sem.at[b])
 
-    for loads in feature_loads:
-        for load in loads:
-            load.wait()
+    own = inputs.at[0, :, pl.ds(0, piece), :]
+    pltpu.make_async_copy(own, own, feature_sem).wait()
     counts_load = pltpu.make_async_copy(counts_hbm, counts, load_sem.at[4])
     counts_load.start()
     places_load = pltpu.make_async_copy(places_hbm, places, load_sem.at[5])
@@ -361,9 +373,8 @@
         load.start()
 
     pl.semaphore_wait(barrier, peers)
-    for h in range(PARTS):
-        for b in range(blocks):
-            gather_start(0, b, h)
+    for b in range(blocks):
+        gather_start(0, b, 0)
 
     tiles[slots] = jnp.zeros((tile, tile), tiles.dtype)
     spots = tile_rows * tile_cols
@@ -391,6 +402,8 @@
         return carry
 
     lax.fori_loop(0, tile_rows, place_row, 0)
+    for b in range(blocks):
+        gather_start(0, b, 1)
     for load in weight_loads:
         load.wait()
 
@@ -407,15 +420,11 @@
     hide(blocks - 1)
     gather_start(1, blocks - 1, 0)
     if blocks > 1:
-        for h in range(known_parts, PARTS):
-            gather_start(1, 0, h)
-    for h in range(1, PARTS):
-        gather_start(1, blocks - 1, h)
-    if blocks > 1:
         for h in range(known_parts):
             gather_wait(1, 0, h)
         for i in range(n_chip):
             early_unit(i)
+    gather_start(1, blocks - 1, 1)
     run_first(1)
     run_rest(1, 0, middle)
     drain(0)
@@ -472,11 +481,11 @@
             flow(0, items), flow(1, items), flow(0, items), flow(1, items),
             flow(0, detours), flow(1, detours),
             scales(items), scales(items), scales(detours),
-            dma((6,)), dma((blocks, PARTS)), dma((blocks,)),
-            dma((2, blocks, PARTS, n_row - 1)), dma((2, blocks, PARTS, n_row - 1)),
-            dma((2, PARTS, n_chip)), dma((2, PARTS, n_chip)),
-            dma((2, items)), dma((2, items)), dma((2, detours)),
-            dma((items,)), dma((items,)), dma((detours,)),
+            dma((6,)), dma(()), dma((blocks,)),
+            dma((2,)), dma((2, blocks, PARTS)),
+            dma((2,)), dma((2, PARTS, n_chip)),
+            dma((2,)), dma((2, blocks, n_chip)), dma((2, detours)),
+            dma(()), dma((blocks, n_chip)), dma((detours,)),
             pltpu.SMEM(tile_counts.shape, jnp.int32), pltpu.VMEM(places.shape, jnp.int32),
             pltpu.VMEM((8, spots), jnp.int32), pltpu.SMEM((8, spots), jnp.int32),
         ],

time: 67.4 us -> 61.9 us (0.918)
  Pallas kernels: 65.3 us -> 59.8 us
    pallas_call x1, Pallas kernels: 65.3 us -> 59.8 us  [shards(): pl.pallas_call(functools.partial(kernel, n_row, n_col, blocks), out_shape...]
where the time goes in v3:
time: 61.9 us; the launch traced here: 61.6 us
  Pallas kernels  59.8 us (97%)
  other arithmetic  1.88 us (3%)
    pallas_call x1, Pallas kernels, shards(): pl.pallas_call(functools.partial(kernel, n_row, n_col, blocks), out_shape...  59.8 us
    max x1, other arithmetic, shards(): return jnp.maximum(second, 0.0)  1.88 us

profile of v3, /device:TPU:0, one launch (start us, length us, event | category | flops | bytes accessed | tf_op | source)
XLA Modules:
  0.0 61.6 jit_solution(2234918800751304247)
XLA Ops:
  0.0 59.8 %shard_map.64 = f32[256,512]{1,0:T(8,128)} custom-call(s32[4,8]{1,0:T(4,128)} %counts_hbm.1, s32[2,128]{1,0:T(2,128)} %bitcast.3, bf16[256,512]{1,0:T(8,128)(2,1)} %features_hbm.1, bf16[128,128,128]{2,1,0:T(8,128)(2,1)} %bitcast.2, f32[512,512]{1,0:T(8,128)} %weight_one_hbm.1, f32[512,512]{1,0:T(8,128)} %weight_two_hbm.1), custom_call_target="tpu_custom_call" | custom-call | tf_op jit(solution)/shard_map/pallas_call | solution.py:467
  59.8 1.9 %broadcast_maximum_fusion = f32[256,512]{1,0:T(8,128)} fusion(f32[256,512]{1,0:T(8,128)} %shard_map.64), kind=kLoop, calls=%fused_computation | loop fusion | flops 131072 | bytes 1048576 | tf_op jit(solution)/shard_map/max | solution.py:496

commit v4 on v3

--- a/solution.py
+++ b/solution.py
@@ -17,10 +17,10 @@
 def kernel(
     n_row, n_col, blocks,
     counts_hbm, places_hbm, features_hbm, tiles_hbm, weight_one_hbm, weight_two_hbm,
-    out_hbm,
-    tiles, dense, weights, inputs, total, result, prod, pair_in,
+    out_ref,
+    tiles, dense, weights, inputs, total, prod, pair_in,
     out0, out1, land0, land1, via0, via1, scale_out, scale_land, scale_via,
-    load_sem, feature_sem, out_sem, gather_send, gather_recv, pair_send, pair_recv,
+    load_sem, feature_sem, gather_send, gather_recv, pair_send, pair_recv,
     link_send, land_recv, via_recv, scale_send, scale_land_recv, scale_via_recv,
     counts, places, inverse_rows, inverse_ref,
 ):
@@ -232,7 +232,7 @@
         )
 
     early = depth - depth // blocks
-    known_parts = PARTS - 1
+    known_parts = PARTS // 2
 
     def unit(layer, u):
         h, i = u // n_chip, lax.rem(u, n_chip)
@@ -321,11 +321,25 @@
 
         lax.fori_loop(0, units + LEAD, body, 0)
 
+    def run_merge(layer):
+        def body(i, carry):
+            d = late_chip(i)
+
+            @pl.when((d != chip) & jnp.logical_not(end_chip))
+            def _():
+                for b in range(1, blocks):
+                    send(layer, b, 0, d)
+
+            return carry
+
+        if blocks > 1:
+            lax.fori_loop(1, n_chip, body, 0)
+
     def run_rest(layer, begin, end):
         def body(w, carry):
             d, h = late_chip(w // PARTS), lax.rem(w, PARTS)
 
-            @pl.when((d != chip) & jnp.logical_not(end_chip & (h == 0)))
+            @pl.when((d != chip) & ((h > 0) | ((w == 0) & jnp.logical_not(end_chip))))
             def _():
                 for b in range(1, blocks):
                     send(layer, b, h, d)
@@ -352,10 +366,6 @@
                 scale_send if scale else link_send.at[layer],
                 (scale_land_recv if scale else land_recv.at[layer]).at[0, 0],
             ).wait_send()
-
-    def out_copy(b):
-        rows = pl.ds(b * sub, sub)
-        return pltpu.make_async_copy(result.at[rows, :], out_hbm.at[rows, :], out_sem.at[b])
 
     own = inputs.at[0, :, pl.ds(0, piece), :]
     pltpu.make_async_copy(own, own, feature_sem).wait()
@@ -409,6 +419,7 @@
 
     middle = jnp.where(end_chip, units, units // 2)
     run_first(0)
+    run_merge(0)
     run_rest(0, 0, middle)
     if blocks > 1:
         settle(0, 0)
@@ -426,19 +437,16 @@
             early_unit(i)
     gather_start(1, blocks - 1, 1)
     run_first(1)
+    run_merge(1)
     run_rest(1, 0, middle)
     drain(0)
     if blocks > 1:
         settle(1, 0)
-        result[0:sub, :] = project(1, 0)
-        out_copy(0).start()
+        out_ref[0:sub, :] = project(1, 0)
     run_rest(1, middle, units)
     drain(1)
     settle(1, blocks - 1)
-    result[(blocks - 1) * sub :, :] = project(1, blocks - 1)
-    out_copy(blocks - 1).start()
-    for b in range(blocks):
-        out_copy(b).wait()
+    out_ref[(blocks - 1) * sub :, :] = project(1, blocks - 1)
 
 
 def shards(n_row, n_col, features, tile_values, tile_places, tile_counts, weight_one, weight_two):
@@ -463,25 +471,24 @@
         return pltpu.VMEM((count, 1, part), jnp.float32)
 
     dma = pltpu.SemaphoreType.DMA
-    any_space = pl.BlockSpec(memory_space=pl.ANY)
+    hbm = pl.BlockSpec(memory_space=pltpu.HBM)
     second = pl.pallas_call(
         functools.partial(kernel, n_row, n_col, blocks),
         out_shape=jax.ShapeDtypeStruct((piece, width), jnp.float32),
-        in_specs=[any_space] * 6,
-        out_specs=any_space,
+        in_specs=[hbm] * 6,
+        out_specs=pl.BlockSpec(memory_space=pltpu.VMEM),
         scratch_shapes=[
             pltpu.VMEM((slots + 1, tile, tile), jnp.bfloat16),
             pltpu.VMEM((rows, depth), jnp.bfloat16),
             pltpu.VMEM((2, width, width), jnp.float32),
             pltpu.VMEM((2, PARTS, depth, part), jnp.bfloat16),
             pltpu.VMEM((blocks, sub, width), jnp.float32),
-            pltpu.VMEM((piece, width), jnp.float32),
             pltpu.VMEM((2, PARTS, n_chip, 2, piece, part), jnp.float32),
             pltpu.VMEM((2, PARTS, n_chip, piece, part), jnp.float32),
             flow(0, items), flow(1, items), flow(0, items), flow(1, items),
             flow(0, detours), flow(1, detours),
             scales(items), scales(items), scales(detours),
-            dma((6,)), dma(()), dma((blocks,)),
+            dma((6,)), dma(()),
             dma((2,)), dma((2, blocks, PARTS)),
             dma((2,)), dma((2, PARTS, n_chip)),
             dma((2,)), dma((2, blocks, n_chip)), dma((2, detours)),
@@ -490,9 +497,12 @@
             pltpu.VMEM((8, spots), jnp.int32), pltpu.SMEM((8, spots), jnp.int32),
         ],
         compiler_params=pltpu.CompilerParams(
-            collective_id=0, has_side_effects=True, vmem_limit_bytes=60 * 1024 * 1024
+            collective_id=0, has_side_effects=True, vmem_limit_bytes=40 * 1024 * 1024
         ),
-    )(tile_counts, places, features, tiles, weight_one, weight_two)
+    )(*(
+        pltpu.with_memory_space_constraint(x, pltpu.HBM)
+        for x in (tile_counts, places, features, tiles, weight_one, weight_two)
+    ))
     return jnp.maximum(second, 0.0)
 
 

time: 61.9 us -> 59.5 us (0.961)
  Pallas kernels: 59.8 us -> 58.5 us
  other arithmetic: 1.88 us -> 0.84 us
    pallas_call x1, Pallas kernels: 59.8 us -> 58.5 us  [shards(): pl.pallas_call(functools.partial(kernel, n_row, n_col, blocks), out_shape...]
    max x1, other arithmetic: 1.88 us -> 0.84 us  [shards(): return jnp.maximum(second, 0.0)]
where the time goes in v4:
time: 59.5 us; the launch traced here: 59.3 us
  Pallas kernels  58.5 us (98%)
  other arithmetic  0.84 us (1%)
    pallas_call x1, Pallas kernels, shards(): pl.pallas_call(functools.partial(kernel, n_row, n_col, blocks), out_shape...  58.5 us

profile of v4, /device:TPU:0, one launch (start us, length us, event | category | flops | bytes accessed | tf_op | source)
XLA Modules:
  0.0 59.3 jit_solution(16440995541173722893)
XLA Ops:
  0.0 58.5 %shard_map.64 = f32[256,512]{1,0:T(8,128)S(1)} custom-call(s32[4,8]{1,0:T(4,128)} %counts_hbm.1, s32[2,128]{1,0:T(2,128)} %bitcast.3, bf16[256,512]{1,0:T(8,128)(2,1)} %features_hbm.1, bf16[128,128,128]{2,1,0:T(8,128)(2,1)} %bitcast.2, f32[512,512]{1,0:T(8,128)} %weight_one_hbm.1, f32[512,512]{1,0:T(8,128)} %weight_two_hbm.1), custom_call_target="tpu_custom_call" | custom-call | tf_op jit(solution)/shard_map/pallas_call | solution.py:475
  58.5 0.8 %broadcast_maximum_fusion = f32[256,512]{1,0:T(8,128)} fusion(f32[256,512]{1,0:T(8,128)S(1)} %shard_map.64), kind=kLoop, calls=%fused_computation | loop fusion | flops 131072 | bytes 1048576 | tf_op jit(solution)/shard_map/max | solution.py:506

commit v5 on v4

--- a/solution.py
+++ b/solution.py
@@ -20,7 +20,7 @@
     out_ref,
     tiles, dense, weights, inputs, total, prod, pair_in,
     out0, out1, land0, land1, via0, via1, scale_out, scale_land, scale_via,
-    load_sem, feature_sem, gather_send, gather_recv, pair_send, pair_recv,
+    wave, load_sem, feature_sem, gather_send, gather_recv, pair_send, pair_recv,
     link_send, land_recv, via_recv, scale_send, scale_land_recv, scale_via_recv,
     counts, places, inverse_rows, inverse_ref,
 ):
@@ -38,14 +38,17 @@
 
     barrier = pltpu.get_barrier_semaphore()
 
-    def greet(step, carry):
-        pl.semaphore_signal(
-            barrier, inc=1, device_id=(row, lax.rem(chip + step, n_chip) * 2 + core),
-            device_id_type=MESH,
-        )
-        return carry
-
-    lax.fori_loop(1, n_chip, greet, 0)
+    def beside(way):
+        return (row, (chip + way) * 2 + core)
+
+    @pl.when(chip > 0)
+    def _():
+        pl.semaphore_signal(barrier, inc=1, device_id=beside(-1), device_id_type=MESH)
+
+    @pl.when(chip < n_chip - 1)
+    def _():
+        pl.semaphore_signal(barrier, inc=1, device_id=beside(1), device_id_type=MESH)
+
     for step in range(1, n_row):
         pl.semaphore_signal(
             barrier, inc=1, device_id=(lax.rem(row + step, n_row), col), device_id_type=MESH
@@ -69,7 +72,8 @@
     for loads in feature_loads:
         for load in loads:
             load.start()
-    peers = n_row - 1 + 1 + n_chip - 1
+    peers = n_row + jnp.where(chip > 0, 1, 0) + jnp.where(chip < n_chip - 1, 1, 0)
+    lower = chip < n_chip // 2
     end_chip = (chip == 0) | (chip == turns)
     neighbour = jnp.where(chip == 0, 1, turns - 1)
 
@@ -94,6 +98,15 @@
     def gather_wait(layer, b, h):
         block = inputs.at[layer, h, pl.ds(0, (n_row - 1) * sub), :]
         whole_wait(block, gather_send.at[layer], gather_recv.at[layer, b, h]).wait_recv()
+
+    def pass_on(way, waits):
+        at = 0 if way > 0 else 1
+        if waits:
+            pl.semaphore_wait(wave.at[at], 1)
+
+        @pl.when((chip < n_chip - 1) if way > 0 else (chip > 0))
+        def _():
+            pl.semaphore_signal(wave.at[at], inc=1, device_id=beside(way), device_id_type=MESH)
 
     def pair_copy(layer, h, d):
         return pltpu.make_async_remote_copy(
@@ -385,6 +398,14 @@
     pl.semaphore_wait(barrier, peers)
     for b in range(blocks):
         gather_start(0, b, 0)
+
+    @pl.when(chip == 0)
+    def _():
+        pass_on(1, False)
+
+    @pl.when(chip == n_chip - 1)
+    def _():
+        pass_on(-1, False)
 
     tiles[slots] = jnp.zeros((tile, tile), tiles.dtype)
     spots = tile_rows * tile_cols
@@ -401,6 +422,15 @@
     inverse_load = pltpu.make_async_copy(inverse_rows, inverse_ref, load_sem.at[3])
     inverse_load.start()
     inverse_load.wait()
+
+    @pl.when(lower & (chip > 0))
+    def _():
+        pass_on(1, True)
+
+    @pl.when(jnp.logical_not(lower) & (chip < n_chip - 1))
+    def _():
+        pass_on(-1, True)
+
     tile_load.wait()
 
     def place_row(i, carry):
@@ -414,6 +444,15 @@
     lax.fori_loop(0, tile_rows, place_row, 0)
     for b in range(blocks):
         gather_start(0, b, 1)
+
+    @pl.when(lower)
+    def _():
+        pass_on(-1, True)
+
+    @pl.when(jnp.logical_not(lower))
+    def _():
+        pass_on(1, True)
+
     for load in weight_loads:
         load.wait()
 
@@ -488,7 +527,7 @@
             flow(0, items), flow(1, items), flow(0, items), flow(1, items),
             flow(0, detours), flow(1, detours),
             scales(items), scales(items), scales(detours),
-            dma((6,)), dma(()),
+            pltpu.SemaphoreType.REGULAR((2,)), dma((6,)), dma(()),
             dma((2,)), dma((2, blocks, PARTS)),
             dma((2,)), dma((2, PARTS, n_chip)),
             dma((2,)), dma((2, blocks, n_chip)), dma((2, detours)),

time: 59.5 us -> 59 us (level)
  Pallas kernels: 58.5 us -> 57.9 us
where the time goes in v5:
time: 59 us; the launch traced here: 58.8 us
  Pallas kernels  57.9 us (98%)
  other arithmetic  0.84 us (1%)
    pallas_call x1, Pallas kernels, shards(): pl.pallas_call(functools.partial(kernel, n_row, n_col, blocks), out_shape...  57.9 us

profile of v5, /device:TPU:0, one launch (start us, length us, event | category | flops | bytes accessed | tf_op | source)
XLA Modules:
  0.0 58.8 jit_solution(7753067051080273763)
XLA Ops:
  0.0 57.9 %shard_map.64 = f32[256,512]{1,0:T(8,128)S(1)} custom-call(s32[4,8]{1,0:T(4,128)} %counts_hbm.1, s32[2,128]{1,0:T(2,128)} %bitcast.3, bf16[256,512]{1,0:T(8,128)(2,1)} %features_hbm.1, bf16[128,128,128]{2,1,0:T(8,128)(2,1)} %bitcast.2, f32[512,512]{1,0:T(8,128)} %weight_one_hbm.1, f32[512,512]{1,0:T(8,128)} %weight_two_hbm.1), custom_call_target="tpu_custom_call" | custom-call | tf_op jit(solution)/shard_map/pallas_call | solution.py:514
  58.0 0.8 %broadcast_maximum_fusion = f32[256,512]{1,0:T(8,128)} fusion(f32[256,512]{1,0:T(8,128)S(1)} %shard_map.64), kind=kLoop, calls=%fused_computation | loop fusion | flops 131072 | bytes 1048576 | tf_op jit(solution)/shard_map/max | solution.py:545

commit v6 on v5

--- a/solution.py
+++ b/solution.py
@@ -12,6 +12,7 @@
 LINK_TYPES = (jnp.int16, jnp.bfloat16)
 TOP = 32766.0
 LEAD = 3
+FILL = 1
 
 
 def kernel(
@@ -82,11 +83,11 @@
         return pltpu.make_async_remote_copy(
             src_ref=block, dst_ref=block,
             send_sem=gather_send.at[layer], recv_sem=gather_recv.at[layer, b, h],
-            device_id=(lax.rem(row + step, n_row), col), device_id_type=MESH,
+            device_id=(row ^ step, col), device_id_type=MESH,
         )
 
     def gather_start(layer, b, h):
-        for step in range(1, n_row):
+        for step in reversed(range(1, n_row)):
             gather_copy(layer, b, h, step).start()
 
     def whole_wait(block, send_sem, recv_sem):
@@ -121,10 +122,16 @@
     def spot_of(b, h, d):
         return (b * PARTS + h) * n_chip + d
 
+    skipped = 2 if n_chip > 3 else 0
+
+    def via_spot(b, h, d):
+        spot = ((b - 1) * PARTS + h) * (n_chip - skipped)
+        return spot + d - jnp.where(lower, skipped, 0)
+
     def link_copy(layer, b, h, d, target, scale, via):
         at, here = spot_of(b, h, d), spot_of(b, h, chip)
         if via:
-            there = spot_of(b - 1, h, d)
+            there = via_spot(b, h, d)
             place = (scale_via if scale else vias[layer]).at[there]
             recv = (scale_via_recv if scale else via_recv.at[layer]).at[there]
         else:
@@ -181,7 +188,7 @@
         return decode(layer, lands[layer][at], scale_land[at])
 
     def take_via(layer, b, h, d):
-        at = spot_of(b - 1, h, d)
+        at = via_spot(b, h, d)
         for scale in both(layer):
             link_copy(layer, b, h, d, partner // 2, scale, True).wait_recv()
         return decode(layer, vias[layer][at], scale_via[at])
@@ -321,7 +328,7 @@
                 def _():
                     send(layer, 0, h, d)
 
-                @pl.when((d != chip) & end_chip & (h == 0))
+                @pl.when((d != chip) & end_chip & (h < FILL))
                 def _():
                     for b in range(1, blocks):
                         send(layer, b, h, d)
@@ -341,7 +348,8 @@
             @pl.when((d != chip) & jnp.logical_not(end_chip))
             def _():
                 for b in range(1, blocks):
-                    send(layer, b, 0, d)
+                    for h in range(FILL):
+                        send(layer, b, h, d)
 
             return carry
 
@@ -352,7 +360,7 @@
         def body(w, carry):
             d, h = late_chip(w // PARTS), lax.rem(w, PARTS)
 
-            @pl.when((d != chip) & ((h > 0) | ((w == 0) & jnp.logical_not(end_chip))))
+            @pl.when((d != chip) & ((h >= FILL) | ((w < PARTS) & jnp.logical_not(end_chip))))
             def _():
                 for b in range(1, blocks):
                     send(layer, b, h, d)
@@ -469,12 +477,13 @@
     settle(0, blocks - 1)
     hide(blocks - 1)
     gather_start(1, blocks - 1, 0)
+    gather_start(1, blocks - 1, 1)
     if blocks > 1:
         for h in range(known_parts):
             gather_wait(1, 0, h)
         for i in range(n_chip):
             early_unit(i)
-    gather_start(1, blocks - 1, 1)
+
     run_first(1)
     run_merge(1)
     run_rest(1, 0, middle)
@@ -501,7 +510,7 @@
     n_chip = n_col // 2
     spots = tile_rows * tile_cols
     items = blocks * PARTS * n_chip
-    detours = max(1, (blocks - 1) * PARTS * n_chip)
+    detours = max(1, (blocks - 1) * PARTS * (n_chip - 2 if n_chip > 3 else n_chip))
 
     def flow(layer, count):
         return pltpu.VMEM((count, sub, part), LINK_TYPES[layer])

time: 59 us -> 58.4 us (0.990)
  no operation moved by 1% of the time
where the time goes in v6:
time: 58.4 us; the launch traced here: 58.2 us
  Pallas kernels  57.4 us (98%)
  other arithmetic  0.84 us (1%)
    pallas_call x1, Pallas kernels, shards(): pl.pallas_call(functools.partial(kernel, n_row, n_col, blocks), out_shape...  57.4 us

profile of v6, /device:TPU:0, one launch (start us, length us, event | category | flops | bytes accessed | tf_op | source)
XLA Modules:
  0.0 58.2 jit_solution(5785683624593590655)
XLA Ops:
  0.0 57.4 %shard_map.64 = f32[256,512]{1,0:T(8,128)S(1)} custom-call(s32[4,8]{1,0:T(4,128)} %counts_hbm.1, s32[2,128]{1,0:T(2,128)} %bitcast.3, bf16[256,512]{1,0:T(8,128)(2,1)} %features_hbm.1, bf16[128,128,128]{2,1,0:T(8,128)(2,1)} %bitcast.2, f32[512,512]{1,0:T(8,128)} %weight_one_hbm.1, f32[512,512]{1,0:T(8,128)} %weight_two_hbm.1), custom_call_target="tpu_custom_call" | custom-call | tf_op jit(solution)/shard_map/pallas_call | solution.py:523
  57.4 0.8 %broadcast_maximum_fusion = f32[256,512]{1,0:T(8,128)} fusion(f32[256,512]{1,0:T(8,128)S(1)} %shard_map.64), kind=kLoop, calls=%fused_computation | loop fusion | flops 131072 | bytes 1048576 | tf_op jit(solution)/shard_map/max | solution.py:554

commit v7 on v6

--- a/solution.py
+++ b/solution.py
@@ -486,12 +486,11 @@
 
     run_first(1)
     run_merge(1)
-    run_rest(1, 0, middle)
+    run_rest(1, 0, units)
     drain(0)
     if blocks > 1:
         settle(1, 0)
         out_ref[0:sub, :] = project(1, 0)
-    run_rest(1, middle, units)
     drain(1)
     settle(1, blocks - 1)
     out_ref[(blocks - 1) * sub :, :] = project(1, blocks - 1)

time: 58.4 us -> 58.4 us (level)
  no operation moved by 1% of the time
where the time goes in v7:
time: 58.4 us; the launch traced here: 58.2 us
  Pallas kernels  57.4 us (98%)
  other arithmetic  0.84 us (1%)
    pallas_call x1, Pallas kernels, shards(): pl.pallas_call(functools.partial(kernel, n_row, n_col, blocks), out_shape...  57.4 us

profile of v7, /device:TPU:0, one launch (start us, length us, event | category | flops | bytes accessed | tf_op | source)
XLA Modules:
  0.0 58.2 jit_solution(13975369733904072824)
XLA Ops:
  0.0 57.4 %shard_map.64 = f32[256,512]{1,0:T(8,128)S(1)} custom-call(s32[4,8]{1,0:T(4,128)} %counts_hbm.1, s32[2,128]{1,0:T(2,128)} %bitcast.3, bf16[256,512]{1,0:T(8,128)(2,1)} %features_hbm.1, bf16[128,128,128]{2,1,0:T(8,128)(2,1)} %bitcast.2, f32[512,512]{1,0:T(8,128)} %weight_one_hbm.1, f32[512,512]{1,0:T(8,128)} %weight_two_hbm.1), custom_call_target="tpu_custom_call" | custom-call | tf_op jit(solution)/shard_map/pallas_call | solution.py:522
  57.4 0.8 %broadcast_maximum_fusion = f32[256,512]{1,0:T(8,128)} fusion(f32[256,512]{1,0:T(8,128)S(1)} %shard_map.64), kind=kLoop, calls=%fused_computation | loop fusion | flops 131072 | bytes 1048576 | tf_op jit(solution)/shard_map/max | solution.py:553

commit v8 on v6

--- a/solution.py
+++ b/solution.py
@@ -136,7 +136,7 @@
             recv = (scale_via_recv if scale else via_recv.at[layer]).at[there]
         else:
             place = (scale_land if scale else lands[layer]).at[here]
-            recv = (scale_land_recv if scale else land_recv.at[layer]).at[b, chip]
+            recv = (scale_land_recv if scale else land_recv.at[layer]).at[0 if b == 0 else 1 + (b - 1) * n_chip + chip]
         return pltpu.make_async_remote_copy(
             src_ref=(scale_out if scale else outs[layer]).at[at], dst_ref=place,
             send_sem=scale_send if scale else link_send.at[layer], recv_sem=recv,
@@ -178,9 +178,13 @@
     def land_wait(layer, b, s):
         for scale in both(layer):
             whole_wait(
-                (scale_land if scale else lands[layer]).at[pl.ds(0, PARTS)],
+                (scale_land if scale else lands[layer]).at[
+                    pl.ds(0, PARTS * turns if b == 0 else PARTS)
+                ],
                 scale_send if scale else link_send.at[layer],
-                (scale_land_recv if scale else land_recv.at[layer]).at[b, s],
+                (scale_land_recv if scale else land_recv.at[layer]).at[
+                    0 if b == 0 else 1 + (b - 1) * n_chip + s
+                ],
             ).wait_recv()
 
     def take_land(layer, b, h, s):
@@ -221,12 +225,16 @@
         for h in range(PARTS):
             total[b, :, h * part : (h + 1) * part] = pair_sum(layer, b, h, chip)
 
+        if b == 0:
+            land_wait(layer, b, 0)
+
         def add(i, carry):
             s = late_chip(i)
 
             @pl.when(sources(b, s))
             def _():
-                land_wait(layer, b, s)
+                if b > 0:
+                    land_wait(layer, b, s)
                 for h in range(PARTS):
                     total[b, :, h * part : (h + 1) * part] += take_land(layer, b, h, s)
 
@@ -385,7 +393,7 @@
             whole_wait(
                 (scale_out if scale else outs[layer]).at[pl.ds(0, blocks * PARTS * turns)],
                 scale_send if scale else link_send.at[layer],
-                (scale_land_recv if scale else land_recv.at[layer]).at[0, 0],
+                (scale_land_recv if scale else land_recv.at[layer]).at[0],
             ).wait_send()
 
     own = inputs.at[0, :, pl.ds(0, piece), :]
@@ -539,8 +547,8 @@
             pltpu.SemaphoreType.REGULAR((2,)), dma((6,)), dma(()),
             dma((2,)), dma((2, blocks, PARTS)),
             dma((2,)), dma((2, PARTS, n_chip)),
-            dma((2,)), dma((2, blocks, n_chip)), dma((2, detours)),
-            dma(()), dma((blocks, n_chip)), dma((detours,)),
+            dma((2,)), dma((2, 1 + (blocks - 1) * n_chip)), dma((2, detours)),
+            dma(()), dma((1 + (blocks - 1) * n_chip,)), dma((detours,)),
             pltpu.SMEM(tile_counts.shape, jnp.int32), pltpu.VMEM(places.shape, jnp.int32),
             pltpu.VMEM((8, spots), jnp.int32), pltpu.SMEM((8, spots), jnp.int32),
         ],

time: 58.4 us -> 58.3 us (level)
  no operation moved by 1% of the time
where the time goes in v8:
time: 58.3 us; the launch traced here: 58.1 us
  Pallas kernels  57.3 us (98%)
  other arithmetic  0.84 us (1%)
    pallas_call x1, Pallas kernels, shards(): pl.pallas_call(functools.partial(kernel, n_row, n_col, blocks), out_shape...  57.3 us

profile of v8, /device:TPU:0, one launch (start us, length us, event | category | flops | bytes accessed | tf_op | source)
XLA Modules:
  0.0 58.1 jit_solution(18285847004452305540)
XLA Ops:
  0.0 57.3 %shard_map.64 = f32[256,512]{1,0:T(8,128)S(1)} custom-call(s32[4,8]{1,0:T(4,128)} %counts_hbm.1, s32[2,128]{1,0:T(2,128)} %bitcast.3, bf16[256,512]{1,0:T(8,128)(2,1)} %features_hbm.1, bf16[128,128,128]{2,1,0:T(8,128)(2,1)} %bitcast.2, f32[512,512]{1,0:T(8,128)} %weight_one_hbm.1, f32[512,512]{1,0:T(8,128)} %weight_two_hbm.1), custom_call_target="tpu_custom_call" | custom-call | tf_op jit(solution)/shard_map/pallas_call | solution.py:531
  57.3 0.8 %broadcast_maximum_fusion = f32[256,512]{1,0:T(8,128)} fusion(f32[256,512]{1,0:T(8,128)S(1)} %shard_map.64), kind=kLoop, calls=%fused_computation | loop fusion | flops 131072 | bytes 1048576 | tf_op jit(solution)/shard_map/max | solution.py:562
